TPU v7x, 32 devices: a 4x4x1 block of a 4x4x8 slice. The times are simulated.
32 devices in a mesh: data: 1 (over z), model: 32 (over y, x, core).
Axes of the slice: x: 4, y: 4, z: 1, core: 2. Of those that a mesh axis runs over, the one named last changes fastest.
The devices are a block of a 4x4x8 slice.
Arguments:
- act_x: bfloat16 [4096, 2048], P('data')
- seg_ids: int32 [4096], P('data')
- gain_one: bfloat16 [2048], replicated
- gain_two: bfloat16 [2048], replicated
- w_qkv: bfloat16 [2048, 6144], P(None, 'model')
- w_out: bfloat16 [32, 64, 2048], P('model')
- w_up: bfloat16 [2048, 8192], P(None, 'model')
- w_down: bfloat16 [8192, 2048], P('model')
- grad_y: bfloat16 [4096, 2048], P('data')
Outputs:
- output 1: bfloat16 [4096, 2048], P('data')
- output 2: bfloat16 [4096, 2048], P('data')
- output 3: bfloat16 [2048, 6144], P('data', 'model')
- output 4: bfloat16 [32, 64, 2048], P(('data', 'model'))
- output 5: bfloat16 [2048, 8192], P('data', 'model')
- output 6: bfloat16 [8192, 2048], P(('data', 'model'))
- output 7: bfloat16 [2048], P('data')
- output 8: bfloat16 [2048], P('data')
All inputs are finite; a program needn't handle non-finite values.
Results may differ from a plain program's by a relative error of at most 0.02.
Values are sent between devices in bfloat16 or wider.
A program may use at most 768 MiB of HBM per device.

v0:
```python
import functools
import jax
import jax.numpy as jnp
from jax import lax
from jax.sharding import PartitionSpec as P

LN_EPS = 1e-5
gelu_tanh = functools.partial(jax.nn.gelu, approximate=True)


def normalize(values):
    values_f32 = values.astype(jnp.float32)
    centered = values_f32 - jnp.mean(values_f32, axis=-1, keepdims=True)
    inv_std = lax.rsqrt(jnp.mean(centered * centered, axis=-1, keepdims=True) + LN_EPS)
    return centered * inv_std, inv_std


def norm_backward(grad_out, x_hat, inv_std, gain_vec):
    d_gain = jnp.sum(grad_out * x_hat, axis=0)
    d_hat = grad_out * gain_vec.astype(jnp.float32)
    d_in = inv_std * (d_hat - jnp.mean(d_hat, axis=-1, keepdims=True)
                      - x_hat * jnp.mean(d_hat * x_hat, axis=-1, keepdims=True))
    return d_in, d_gain


def visible_keys(q_pos, k_pos, q_seg, k_seg):
    return (q_pos[:, None] >= k_pos[None, :]) & (q_seg[:, None] == k_seg[None, :])


def attention_fwd(q_rows, k_rows, v_rows, key_mask):
    q_scale = q_rows.shape[-1] ** -0.5
    scores = jnp.einsum("shd,thd->hst", q_rows, k_rows, preferred_element_type=jnp.float32) * q_scale
    scores = jnp.where(key_mask[None], scores, -1e30)
    prob_f32 = jax.nn.softmax(scores, axis=-1)
    prob_bf = prob_f32.astype(jnp.bfloat16)
    attn_rows = jnp.einsum("hst,thd->shd", prob_bf, v_rows, preferred_element_type=jnp.float32).astype(jnp.bfloat16)
    return attn_rows, prob_f32, prob_bf


def attention_bwd(d_rows, q_rows, k_rows, v_rows, prob_f32, prob_bf):
    q_scale = q_rows.shape[-1] ** -0.5
    d_prob = jnp.einsum("shd,thd->hst", d_rows, v_rows, preferred_element_type=jnp.float32)
    d_prob = d_prob.astype(jnp.bfloat16).astype(jnp.float32)
    d_scores = prob_f32 * (d_prob - jnp.sum(prob_f32 * d_prob, axis=-1, keepdims=True))
    d_scores = (d_scores * q_scale).astype(jnp.bfloat16)
    d_query = jnp.einsum("hst,thd->shd", d_scores, k_rows, preferred_element_type=jnp.float32).astype(jnp.bfloat16)
    d_key = jnp.einsum("hst,shd->thd", d_scores, q_rows, preferred_element_type=jnp.float32).astype(jnp.bfloat16)
    d_value = jnp.einsum("hst,shd->thd", prob_bf, d_rows, preferred_element_type=jnp.float32).astype(jnp.bfloat16)
    return d_query, d_key, d_value


def solution(mesh):
    def local_layer(act_x, seg_ids, gain_one, gain_two, w_qkv, w_out, w_up, w_down, grad_y):
        tokens = act_x.shape[0]
        local_heads, head_dim = w_out.shape[0], w_out.shape[1]
        positions = lax.iota(jnp.int32, tokens)
        key_mask = visible_keys(positions, positions, seg_ids, seg_ids)

        hat_one, inv_one = normalize(act_x)
        normed_one = (hat_one * gain_one.astype(jnp.float32)).astype(jnp.bfloat16)
        qkv_rows = jnp.dot(normed_one, w_qkv, preferred_element_type=jnp.float32).astype(jnp.bfloat16)
        qkv_rows = qkv_rows.reshape(tokens, local_heads, 3, head_dim)
        q_rows = qkv_rows[:, :, 0]
        k_rows = qkv_rows[:, :, 1]
        v_rows = qkv_rows[:, :, 2]
        attn_rows, prob_f32, prob_bf = attention_fwd(q_rows, k_rows, v_rows, key_mask)
        part_one = jnp.einsum("shd,hde->se", attn_rows, w_out, preferred_element_type=jnp.float32).astype(jnp.bfloat16)
        sum_one = lax.psum(part_one, "model")
        resid_rows = (act_x.astype(jnp.float32) + sum_one.astype(jnp.float32)).astype(jnp.bfloat16)
        hat_two, inv_two = normalize(resid_rows)
        normed_two = (hat_two * gain_two.astype(jnp.float32)).astype(jnp.bfloat16)
        pre_act = jnp.dot(normed_two, w_up, preferred_element_type=jnp.float32)
        act_vals, gelu_pull = jax.vjp(gelu_tanh, pre_act)
        hidden = act_vals.astype(jnp.bfloat16)
        part_two = jnp.dot(hidden, w_down, preferred_element_type=jnp.float32).astype(jnp.bfloat16)
        sum_two = lax.psum(part_two, "model")
        layer_out = (resid_rows.astype(jnp.float32) + sum_two.astype(jnp.float32)).astype(jnp.bfloat16)

        d_hidden = jnp.einsum("se,fe->sf", grad_y, w_down, preferred_element_type=jnp.float32).astype(jnp.bfloat16)
        d_down = jnp.einsum("sf,se->fe", hidden, grad_y, preferred_element_type=jnp.float32).astype(jnp.bfloat16)
        d_pre = gelu_pull(d_hidden.astype(jnp.float32))[0].astype(jnp.bfloat16)
        d_up = jnp.einsum("sh,sf->hf", normed_two, d_pre, preferred_element_type=jnp.float32).astype(jnp.bfloat16)
        part_three = jnp.einsum("sf,hf->sh", d_pre, w_up, preferred_element_type=jnp.float32).astype(jnp.bfloat16)
        d_normed_two = lax.psum(part_three, "model").astype(jnp.float32)
        d_in_two, d_gain_two = norm_backward(d_normed_two, hat_two, inv_two, gain_two)
        d_resid = (grad_y.astype(jnp.float32) + d_in_two).astype(jnp.bfloat16)
        d_wout = jnp.einsum("shd,se->hde", attn_rows, d_resid, preferred_element_type=jnp.float32).astype(jnp.bfloat16)
        d_attn = jnp.einsum("se,hde->shd", d_resid, w_out, preferred_element_type=jnp.float32).astype(jnp.bfloat16)
        d_query, d_key, d_value = attention_bwd(d_attn, q_rows, k_rows, v_rows, prob_f32, prob_bf)
        d_qkv = jnp.stack([d_query, d_key, d_value], axis=2).reshape(tokens, 3 * local_heads * head_dim)
        d_wqkv = jnp.einsum("sh,sc->hc", normed_one, d_qkv, preferred_element_type=jnp.float32).astype(jnp.bfloat16)
        part_four = jnp.einsum("sc,hc->sh", d_qkv, w_qkv, preferred_element_type=jnp.float32).astype(jnp.bfloat16)
        d_normed_one = lax.psum(part_four, "model").astype(jnp.float32)
        d_in_one, d_gain_one = norm_backward(d_normed_one, hat_one, inv_one, gain_one)
        grad_x = (d_resid.astype(jnp.float32) + d_in_one).astype(jnp.bfloat16)
        return (layer_out, grad_x, d_wqkv, d_wout, d_up, d_down,
                d_gain_one.astype(jnp.bfloat16), d_gain_two.astype(jnp.bfloat16))

    in_specs = (P("data", None), P("data"), P(None), P(None), P(None, "model"),
                P("model", None, None), P(None, "model"), P("model", None), P("data", None))
    out_specs = (P("data", None), P("data", None), P("data", "model"), P(("data", "model"), None, None),
                 P("data", "model"), P(("data", "model"), None), P("data"), P("data"))
    return jax.shard_map(local_layer, mesh=mesh, in_specs=in_specs, out_specs=out_specs, check_vma=False)
```

profile of v0, /device:TPU:97, one launch (start us, length us, event | category | flops | bytes accessed | tf_op | source)
XLA Modules:
  0.0 1036.5 jit_solution(8195752569449658969)
XLA Ops:
  8.1 7.2 convert_reduce_fusion.1
  18.0 6.5 fusion.32
  24.6 6.4 fusion.27
  42.5 25.8 %fusion.73 = (f32[4096]{0:T(1024)S(1)}, f32[4096,4096]{0,1:T(8,128)}) fusion(bf16[4096,1,3,64]{0,3,2,1:T(8,128)(2,1)S(1)} %bitcast.84, s32[4096]{0:T(1024)S(1)} %copy-done.26), kind=kOutput, calls=%fused_computation.108 | convolution fusion | flops 2248142848 | bytes 68206592 | tf_op jit(solution)/shard_map/shd,thd->hst/dot_general | solution.py:32
  68.3 21.3 %fusion.6 = f32[4096]{0:T(1024)S(1)} fusion(f32[4096,4096]{0,1:T(8,128)} %get-tuple-element.19, f32[4096]{0:T(1024)S(1)} %get-tuple-element.18), kind=kLoop, calls=%fused_computation.11 | loop fusion | flops 33550336 | bytes 67141632 | tf_op jit(solution)/shard_map/reduce_sum | solution.py:34
  89.6 23.9 %fusion.53 = bf16[4096,64]{0,1:T(8,128)(2,1)S(1)} fusion(bf16[4096,1,3,64]{0,3,2,1:T(8,128)(2,1)S(1)} %bitcast.85, f32[4096,4096]{0,1:T(8,128)} %get-tuple-element.19, f32[4096]{0:T(1024)S(1)} %fusion.6, f32[4096]{0:T(1024)S(1)} %get-tuple-element.18), kind=kOutput, calls=%fused_computation.76 | convolution fusion | flops 2198077440 | bytes 68190208 | tf_op jit(solution)/shard_map/hst,thd->shd/dot_general | solution.py:36
  113.5 8.5 convolution_convert_fusion.2
  122.2 170.4 %all-reduce.5.cloned.1.call-done = bf16[4096,2048]{1,0:T(8,128)(2,1)} async-done(((bf16[4096,2048]{1,0:T(8,128)(2,1)}), bf16[4096,2048]{1,0:T(8,128)(2,1)}) %all-reduce.5.cloned.1.call-update) | async-done | bytes 16777232 | tf_op jit(solution)/shard_map/psum | solution.py:68
  292.6 13.5 %convert_reduce_fusion = (f32[4096]{0:T(1024)S(1)}, bf16[4096,2048]{1,0:T(8,128)(2,1)S(1)}) fusion(bf16[4096,2048]{1,0:T(8,128)(2,1)} %all-reduce.5.cloned.1.call-done, bf16[4096,2048]{1,0:T(8,128)(2,1)} %param.9), kind=kLoop, calls=%fused_computation.14 | loop fusion | flops 50327552 | bytes 50348032 | tf_op jit(solution)/shard_map/reduce_sum | solution.py:13
  306.2 6.6 fusion.26
  312.8 9.2 fusion.21
  322.1 8.3 fusion.74
  332.5 7.1 fusion.59
  339.6 8.2 convolution_convert_fusion.3
  349.0 11.1 %convolution_convert_fusion.4 = bf16[4096,2048]{1,0:T(8,128)(2,1)} fusion(bf16[256,2048]{1,0:T(8,128)(2,1)S(1)} %copy-done.13, f32[4096,256]{1,0:T(8,128)} %copy-done.6), kind=kOutput, calls=%fused_computation.62 | convolution fusion | flops 4312793088 | bytes 22020096 | tf_op jit(solution)/shard_map/dot_general | solution.py:75
  360.2 154.9 %all-reduce.7.cloned.1.call-done = bf16[4096,2048]{1,0:T(8,128)(2,1)} async-done(((bf16[4096,2048]{1,0:T(8,128)(2,1)}), bf16[4096,2048]{1,0:T(8,128)(2,1)}) %all-reduce.7.cloned.1.call-update) | async-done | bytes 16777232 | tf_op jit(solution)/shard_map/psum | solution.py:84
  515.1 19.1 %fusion.34 = (bf16[2048]{0:T(1024)(128)(2,1)}, f32[4096]{0:T(1024)S(1)}, f32[4096]{0:T(1024)S(1)}) fusion(bf16[4096,2048]{1,0:T(8,128)(2,1)} %copy-done.3, bf16[4096,2048]{1,0:T(8,128)(2,1)} %all-reduce.7.cloned.1.call-done, f32[4096]{0:T(1024)S(1)} %add_rsqrt_fusion, f32[4096]{0:T(1024)S(1)} %broadcast_multiply_fusion.4, f32[2048]{0:T(1024)S(1)} %convert_element_type.168), kind=kLoop, calls=%fused_computation.49 | loop fusion | flops 83875840 | bytes 33632256 | tf_op jit(solution)/shard_map/reduce_sum | solution.py:19
  534.2 26.3 %fusion.25 = bf16[4096,2048]{1,0:T(8,128)(2,1)} fusion(bf16[4096,2048]{1,0:T(8,128)(2,1)} %copy-done.3, bf16[4096,2048]{1,0:T(8,128)(2,1)} %all-reduce.7.cloned.1.call-done, bf16[4096,2048]{1,0:T(8,128)(2,1)} %param.17, f32[4096]{0:T(1024)S(1)} %get-tuple-element.22, f32[4096]{0:T(1024)S(1)} %get-tuple-element.23, f32[2048]{0:T(1024)S(1)} %convert_element_type.168, ...), kind=kLoop, calls=%fused_computation.40 | loop fusion | flops 100663296 | bytes 67182592 | tf_op jit(solution)/shard_map/convert_element_type | solution.py:86
  560.5 10.9 %convolution_convert_fusion.9 = bf16[4096,64]{0,1:T(8,128)(2,1)S(1)} fusion(bf16[4096,2048]{1,0:T(8,128)(2,1)} %fusion.25, bf16[1,64,2048]{2,1,0:T(8,128)(2,1)S(1)} %copy-done.11), kind=kOutput, calls=%fused_computation.73 | convolution fusion | flops 1074003968 | bytes 17563648 | tf_op jit(solution)/shard_map/se,hde->shd/dot_general | solution.py:88
  571.4 24.5 %fusion.50 = bf16[4096,1,1,64]{0,3,2,1:T(8,128)(2,1)} fusion(bf16[4096,64]{0,1:T(8,128)(2,1)S(1)} %convolution_convert_fusion.9, f32[4096,4096]{0,1:T(8,128)} %get-tuple-element.19, f32[4096]{0:T(1024)S(1)} %fusion.6, f32[4096]{0:T(1024)S(1)} %get-tuple-element.18), kind=kOutput, calls=%fused_computation.75 | convolution fusion | flops 2198077440 | bytes 68190208 | tf_op jit(solution)/shard_map/hst,shd->thd/dot_general | solution.py:48
  596.0 35.2 %fusion = (f32[4096]{0:T(1024)S(1)}, bf16[4096,4096]{0,1:T(8,128)(2,1)}) fusion(f32[4096]{0:T(1024)S(1)} %fusion.6, f32[4096,4096]{0,1:T(8,128)} %get-tuple-element.19, f32[4096]{0:T(1024)S(1)} %get-tuple-element.18, bf16[4096,64]{0,1:T(8,128)(2,1)S(1)} %convolution_convert_fusion.9, bf16[4096,1,3,64]{0,3,2,1:T(8,128)(2,1)S(1)} %bitcast.86), kind=kOutput, calls=%fused_computation.2 | convolution fusion | flops 2248142848 | bytes 101761024 | tf_op jit(solution)/shard_map/shd,thd->hst/dot_general | solution.py:42
  631.2 43.3 %fusion.3 = bf16[4096,4096]{0,1:T(8,128)(2,1)} fusion(bf16[4096,4096]{0,1:T(8,128)(2,1)} %get-tuple-element.21, f32[4096]{0:T(1024)S(1)} %get-tuple-element.20, f32[4096]{0:T(1024)S(1)} %fusion.6, f32[4096,4096]{0,1:T(8,128)} %get-tuple-element.19, f32[4096]{0:T(1024)S(1)} %get-tuple-element.18), kind=kLoop, calls=%fused_computation.5 | loop fusion | flops 117440512 | bytes 134266880 | tf_op jit(solution)/shard_map/convert_element_type | solution.py:45
  674.5 15.5 %fusion.56 = bf16[4096,1,1,64]{0,3,2,1:T(8,128)(2,1)S(1)} fusion(bf16[4096,4096]{0,1:T(8,128)(2,1)} %fusion.3, bf16[4096,1,3,64]{0,3,2,1:T(8,128)(2,1)S(1)} %bitcast.87), kind=kOutput, calls=%fused_computation.77 | convolution fusion | flops 2147745792 | bytes 34603008 | tf_op jit(solution)/shard_map/hst,shd->thd/dot_general | solution.py:47
  690.0 13.7 %fusion.49 = bf16[4096,1,1,64]{0,3,2,1:T(8,128)(2,1)S(1)} fusion(bf16[4096,4096]{0,1:T(8,128)(2,1)} %fusion.3, bf16[4096,1,3,64]{0,3,2,1:T(8,128)(2,1)S(1)} %bitcast.88), kind=kOutput, calls=%fused_computation.74 | convolution fusion | flops 2147745792 | bytes 34603008 | tf_op jit(solution)/shard_map/hst,thd->shd/dot_general | solution.py:46
  704.0 8.6 convolution_convert_fusion.1
  712.6 12.5 %convolution_convert_fusion.11 = bf16[2048,256]{1,0:T(8,128)(2,1)} fusion(bf16[4096,2048]{1,0:T(8,128)(2,1)} %fusion.21, bf16[4096,256]{1,0:T(8,128)(2,1)} %copy-done.10), kind=kOutput, calls=%fused_computation.90 | convolution fusion | flops 4295491584 | bytes 19922944 | tf_op jit(solution)/shard_map/sh,sf->hf/dot_general | solution.py:82
  725.1 9.6 convolution_convert_fusion.10
  738.5 8.7 convolution_convert_fusion.12
  747.2 215.4 %all-reduce.9.cloned.1.call-done = (bf16[4096,2048]{1,0:T(8,128)(2,1)}, bf16[4096,2048]{1,0:T(8,128)(2,1)}) async-done(((bf16[4096,2048]{1,0:T(8,128)(2,1)}, bf16[4096,2048]{1,0:T(8,128)(2,1)}), (bf16[4096,2048]{1,0:T(8,128)(2,1)}, bf16[4096,2048]{1,0:T(8,128)(2,1)})) %all-reduce.9.cloned.1.call-update) | async-done | bytes 33554448 | tf_op jit(solution)/shard_map/psum | solution.py:76
  962.6 22.4 %fusion.38 = bf16[4096,2048]{1,0:T(8,128)(2,1)} fusion(bf16[4096,2048]{1,0:T(8,128)(2,1)} %copy-done.3, bf16[4096,2048]{1,0:T(8,128)(2,1)} %get-tuple-element.14), kind=kLoop, calls=%fused_computation.53 | loop fusion | flops 33554432 | bytes 50331648 | tf_op jit(solution)/shard_map/convert_element_type | solution.py:77
  985.0 18.1 %fusion.36 = (bf16[2048]{0:T(1024)(128)(2,1)}, f32[4096]{0:T(1024)S(1)}, f32[4096]{0:T(1024)S(1)}) fusion(bf16[4096,2048]{1,0:T(8,128)(2,1)} %param.9, bf16[4096,2048]{1,0:T(8,128)(2,1)S(1)} %copy-done.4, f32[4096]{0:T(1024)S(1)} %copy-done.22, f32[4096]{0:T(1024)S(1)} %copy-done.20, f32[2048]{0:T(1024)S(1)} %copy-done.24), kind=kLoop, calls=%fused_computation.51 | loop fusion | flops 83875840 | bytes 33632256 | tf_op jit(solution)/shard_map/reduce_sum | solution.py:19
  1003.1 26.6 %fusion.31 = bf16[4096,2048]{1,0:T(8,128)(2,1)} fusion(bf16[4096,2048]{1,0:T(8,128)(2,1)} %param.9, bf16[4096,2048]{1,0:T(8,128)(2,1)} %get-tuple-element.15, bf16[4096,2048]{1,0:T(8,128)(2,1)} %fusion.25, f32[4096]{0:T(1024)S(1)} %broadcast_multiply_fusion, f32[4096]{0:T(1024)S(1)} %broadcast_multiply_fusion.1, f32[2048]{0:T(1024)S(1)} %copy-done.24, ...), kind=kLoop, calls=%fused_computation.46 | loop fusion | flops 100663296 | bytes 67182592 | tf_op jit(solution)/shard_map/convert_element_type | solution.py:95
  (90 shorter events, 22.5 us)
Async XLA Ops:
  7.2 314.9 %copy-start = (bf16[2048,256]{1,0:T(8,128)(2,1)S(1)}, bf16[2048,256]{1,0:T(8,128)(2,1)}, u32[]{:S(2)}) copy-start(bf16[2048,256]{1,0:T(8,128)(2,1)} %param.15) | copy-start | bytes 3145732
  7.2 285.4 %all-reduce.5.cloned.1.call-start = ((), (), s32[]{:S(2)}) async-start(), calls=%async_computation | async-start | bytes 33554432 | tf_op jit(solution)/shard_map/psum | solution.py:68
  7.3 10.8 %copy-start.2 = (bf16[4096,2048]{1,0:T(8,128)(2,1)S(1)}, bf16[4096,2048]{1,0:T(8,128)(2,1)}, u32[]{:S(2)}) copy-start(bf16[4096,2048]{1,0:T(8,128)(2,1)} %param.9) | copy-start | bytes 50331652
  8.1 16.5 %copy-start.23 = (f32[2048]{0:T(1024)}, f32[2048]{0:T(1024)S(1)}, u32[]{:S(2)}) copy-start(f32[2048]{0:T(1024)S(1)} %convert_element_type.157) | copy-start | bytes 24580
  18.0 13.1 %copy-start.19 = (f32[4096]{0:T(1024)}, f32[4096]{0:T(1024)S(1)}, u32[]{:S(2)}) copy-start(f32[4096]{0:T(1024)S(1)} %broadcast_multiply_fusion.5) | copy-start | bytes 49156
  24.6 12.2 %copy-start.16 = (bf16[2048,192]{0,1:T(8,128)(2,1)S(1)}, bf16[2048,192]{0,1:T(8,128)(2,1)}, u32[]{:S(2)}) copy-start(bf16[2048,192]{0,1:T(8,128)(2,1)} %param.13) | copy-start | bytes 2359300
  42.5 47.1 %copy-start.14 = (bf16[4096,192]{0,1:T(8,128)(2,1)}, bf16[4096,192]{0,1:T(8,128)(2,1)S(1)}, u32[]{:S(2)}) copy-start(bf16[4096,192]{0,1:T(8,128)(2,1)S(1)} %convolution_convert_fusion.6) | copy-start | bytes 4718596
  89.6 23.9 %copy-start.11 = (bf16[1,64,2048]{2,1,0:T(8,128)(2,1)S(1)}, bf16[1,64,2048]{2,1,0:T(8,128)(2,1)}, u32[]{:S(2)}) copy-start(bf16[1,64,2048]{2,1,0:T(8,128)(2,1)} %param.14) | copy-start | bytes 786436
  113.5 8.6 copy-start.8
  113.5 8.7 copy-start.25
  122.1 392.9 %all-reduce.7.cloned.1.call-start = ((), (), s32[]{:S(2)}) async-start(), calls=%async_computation.1 | async-start | bytes 33554432 | tf_op jit(solution)/shard_map/psum | solution.py:84
  312.8 19.6 %slice-start.4 = ((s8[16777216]{0:T(1024)(128)(4,1)}), s8[4194304]{0:T(1024)(128)(4,1)S(1)}, s32[]{:S(2)}) async-start(s8[16777216]{0:T(1024)(128)(4,1)} %bitcast.80), calls=%async_computation.7 | async-start | bytes 8388608
  312.8 19.6 %slice-start.5 = ((s8[16777216]{0:T(1024)(128)(4,1)}), s8[4194304]{0:T(1024)(128)(4,1)S(1)}, s32[]{:S(2)}) async-start(s8[16777216]{0:T(1024)(128)(4,1)} %bitcast.80), calls=%async_computation.8 | async-start | bytes 8388608
  322.1 10.4 %slice-start.6 = ((s8[16777216]{0:T(1024)(128)(4,1)}), s8[4194304]{0:T(1024)(128)(4,1)S(1)}, s32[]{:S(2)}) async-start(s8[16777216]{0:T(1024)(128)(4,1)} %bitcast.80), calls=%async_computation.9 | async-start | bytes 8388608
  322.1 10.4 %slice-start.7 = ((s8[16777216]{0:T(1024)(128)(4,1)}), s8[4194304]{0:T(1024)(128)(4,1)S(1)}, s32[]{:S(2)}) async-start(s8[16777216]{0:T(1024)(128)(4,1)} %bitcast.80), calls=%async_computation.10 | async-start | bytes 8388608
  322.1 10.4 %copy-start.12 = (bf16[256,2048]{1,0:T(8,128)(2,1)S(1)}, bf16[256,2048]{1,0:T(8,128)(2,1)}, u32[]{:S(2)}) copy-start(bf16[256,2048]{1,0:T(8,128)(2,1)} %param.16) | copy-start | bytes 3145732
  339.6 8.3 copy-start.10
  347.9 614.7 %all-reduce.9.cloned.1.call-start = ((), (), s32[]{:S(2)}) async-start(), calls=%async_computation.2 | async-start | bytes 67108864 | tf_op jit(solution)/shard_map/psum | solution.py:76
  571.4 24.6 %copy-start.15 = (bf16[4096,192]{0,1:T(8,128)(2,1)S(1)}, bf16[4096,192]{0,1:T(8,128)(2,1)}, u32[]{:S(2)}) copy-start(bf16[4096,192]{0,1:T(8,128)(2,1)} %copy-done.14) | copy-start | bytes 4718596
  690.0 13.8 %copy-start.18 = (bf16[4096,1,1,64]{0,3,2,1:T(8,128)(2,1)S(1)}, bf16[4096,1,1,64]{0,3,2,1:T(8,128)(2,1)}, u32[]{:S(2)}) copy-start(bf16[4096,1,1,64]{0,3,2,1:T(8,128)(2,1)} %fusion.50) | copy-start | bytes 1572868
  690.0 13.9 %copy-start.17 = (bf16[2048,192]{0,1:T(8,128)(2,1)S(1)}, bf16[2048,192]{0,1:T(8,128)(2,1)}, u32[]{:S(2)}) copy-start(bf16[2048,192]{0,1:T(8,128)(2,1)} %param.13) | copy-start | bytes 2359300
  712.6 12.5 %copy-start.7 = (f32[4096,256]{1,0:T(8,128)S(1)}, f32[4096,256]{1,0:T(8,128)}, u32[]{:S(2)}) copy-start(f32[4096,256]{1,0:T(8,128)} %copy-done.6) | copy-start | bytes 12582916
  712.6 22.2 %slice-start = ((s8[16777216]{0:T(1024)(128)(4,1)}), s8[4194304]{0:T(1024)(128)(4,1)S(1)}, s32[]{:S(2)}) async-start(s8[16777216]{0:T(1024)(128)(4,1)} %bitcast.78), calls=%async_computation.3 | async-start | bytes 8388608
  712.6 22.1 %slice-start.1 = ((s8[16777216]{0:T(1024)(128)(4,1)}), s8[4194304]{0:T(1024)(128)(4,1)S(1)}, s32[]{:S(2)}) async-start(s8[16777216]{0:T(1024)(128)(4,1)} %bitcast.78), calls=%async_computation.4 | async-start | bytes 8388608
  712.6 22.1 %slice-start.2 = ((s8[16777216]{0:T(1024)(128)(4,1)}), s8[4194304]{0:T(1024)(128)(4,1)S(1)}, s32[]{:S(2)}) async-start(s8[16777216]{0:T(1024)(128)(4,1)} %bitcast.78), calls=%async_computation.5 | async-start | bytes 8388608
  725.1 9.6 slice-start.3
  725.1 9.6 copy-start.9
  962.6 22.4 %copy-start.4 = (bf16[4096,2048]{1,0:T(8,128)(2,1)S(1)}, bf16[4096,2048]{1,0:T(8,128)(2,1)}, u32[]{:S(2)}) copy-start(bf16[4096,2048]{1,0:T(8,128)(2,1)} %get-tuple-element.15) | copy-start | bytes 50331652
  962.6 22.4 %copy-start.20 = (f32[4096]{0:T(1024)S(1)}, f32[4096]{0:T(1024)}, u32[]{:S(2)}) copy-start(f32[4096]{0:T(1024)} %copy-done.19) | copy-start | bytes 49156
  962.6 22.4 %copy-start.22 = (f32[4096]{0:T(1024)S(1)}, f32[4096]{0:T(1024)}, u32[]{:S(2)}) copy-start(f32[4096]{0:T(1024)} %copy-done.21) | copy-start | bytes 49156
  962.6 22.4 %copy-start.24 = (f32[2048]{0:T(1024)S(1)}, f32[2048]{0:T(1024)}, u32[]{:S(2)}) copy-start(f32[2048]{0:T(1024)} %copy-done.23) | copy-start | bytes 24580
  1003.1 26.6 %copy-start.1 = (bf16[2048,256]{1,0:T(8,128)(2,1)S(1)}, bf16[2048,256]{1,0:T(8,128)(2,1)}, u32[]{:S(2)}) copy-start(bf16[2048,256]{1,0:T(8,128)(2,1)} %param.15) | copy-start | bytes 3145732
  (6 other events, 27.8 us)
Sparse Core Ops, SparseCore 0:
  122.3 170.3 all-reduce.4
  348.0 167.0 all-reduce.6
  712.7 249.8 all-reduce.8
where the time goes:
time: 1050 us; the launch traced here: 1040 us
  waiting for transfers between devices  541 us (52%)
  matrix products  242 us (23%)
  other arithmetic  228 us (22%)
  between operations  14.4 us (1%)
  local copies, waits for them, and re-layouts  11.7 us (1%)
    psum x1, waiting for transfers between devices, local_layer(): sum_two = lax.psum(part_two, 'model')  215 us
    psum x1, waiting for transfers between devices, local_layer(): sum_one = lax.psum(part_one, 'model')  170 us
    psum x1, waiting for transfers between devices, local_layer(): d_normed_two = lax.psum(part_three, 'model').astype(jnp.float32)  155 us
    convert_element_type x1, other arithmetic, attention_bwd(): d_scores = (d_scores * q_scale).astype(jnp.bfloat16)  43.3 us
    reduce_sum x2, other arithmetic, norm_backward(): d_gain = jnp.sum(grad_out * x_hat, axis=0)  37.2 us
    dot_general x1, matrix products, attention_bwd(): jnp.einsum('shd,thd->hst', d_rows, v_rows, preferred_element_type=jnp.flo...  35.2 us
    convert_element_type x1, other arithmetic, local_layer(): grad_x = (d_resid.astype(jnp.float32) + d_in_one).astype(jnp.bfloat16)  26.6 us
    convert_element_type x1, other arithmetic, local_layer(): d_resid = (grad_y.astype(jnp.float32) + d_in_two).astype(jnp.bfloat16)  26.3 us
  transfers between devices with their start and end apart: 3, of which 3 were waited for; matrix products, arithmetic and copies ran while one was open for 4% of the time, Pallas kernels for 0%

commit v1 on v0

v1 whole, which is shorter than its diff:
```python
import functools
import math
import jax
import jax.numpy as jnp
from jax import lax
from jax.experimental import pallas as pl
from jax.experimental.pallas import tpu as pltpu
from jax.sharding import PartitionSpec as P

LN_EPS = 1e-5
VMEM_LIMIT = 60 * 1024 * 1024
BQ = 256
BK = 512
NEG = -1e30


def ln_qkv_kernel(x_ref, g_ref, w_ref, a_ref, qkv_ref):
    x = x_ref[...].astype(jnp.float32)
    centered = x - jnp.mean(x, axis=-1, keepdims=True)
    inv_std = lax.rsqrt(jnp.mean(centered * centered, axis=-1, keepdims=True) + LN_EPS)
    a = (centered * inv_std * g_ref[...].astype(jnp.float32)).astype(jnp.bfloat16)
    a_ref[...] = a
    qkv_ref[...] = jnp.dot(a, w_ref[...], preferred_element_type=jnp.float32).astype(jnp.bfloat16)


def ln_qkv(x, gain, w):
    tokens, width = x.shape
    cols = w.shape[1]
    rows = 512
    return pl.pallas_call(
        ln_qkv_kernel,
        grid=(tokens // rows,),
        in_specs=[pl.BlockSpec((rows, width), lambda i: (i, 0)),
                  pl.BlockSpec((1, width), lambda i: (0, 0)),
                  pl.BlockSpec((width, cols), lambda i: (0, 0))],
        out_specs=[pl.BlockSpec((rows, width), lambda i: (i, 0)),
                   pl.BlockSpec((rows, cols), lambda i: (i, 0))],
        out_shape=[jax.ShapeDtypeStruct((tokens, width), jnp.bfloat16),
                   jax.ShapeDtypeStruct((tokens, cols), jnp.bfloat16)],
        compiler_params=pltpu.CompilerParams(vmem_limit_bytes=VMEM_LIMIT),
        cost_estimate=pl.CostEstimate(flops=2 * tokens * width * cols, bytes_accessed=4 * tokens * width,
                                      transcendentals=0),
        name="ln_qkv",
    )(x, gain[None, :], w)


def _mask(i, j, start):
    shape = (BQ, BK)
    row = lax.broadcasted_iota(jnp.int32, shape, 0) + i * BQ
    col = lax.broadcasted_iota(jnp.int32, shape, 1) + j * BK
    return (col <= row) & (col >= start)


def _lanes(op, value):
    out = value[:, 0:128]
    for t in range(1, value.shape[1] // 128):
        out = op(out, value[:, t * 128:(t + 1) * 128])
    return out


def _kdot(a, b):
    return lax.dot_general(a, b, (((1,), (1,)), ((), ())), preferred_element_type=jnp.float32)


def attn_fwd_kernel(head_dim, lo_ref, qkv_ref, start_ref, o_ref, lse_ref, k_scr, v_scr, strip, stat):
    i = pl.program_id(0)
    scale2 = head_dim ** -0.5 * math.log2(math.e)

    @pl.when(i == 0)
    def _():
        k_scr[...] = qkv_ref[:, head_dim:2 * head_dim]
        v_scr[...] = qkv_ref[:, 2 * head_dim:3 * head_dim]

    q = qkv_ref[pl.ds(pl.multiple_of(i * BQ, BQ), BQ), 0:head_dim]
    start = start_ref[...]
    lo = lo_ref[i]
    hi = (i * BQ + BQ - 1) // BK + 1

    def cols(j):
        return pl.ds(pl.multiple_of(j * BK, BK), BK)

    stat[...] = jnp.full_like(stat, NEG)

    @pl.loop(lo, hi)
    def _(j):
        s = jnp.where(_mask(i, j, start), _kdot(q, k_scr[cols(j), :]), NEG)
        strip[:, cols(j)] = s
        stat[...] = jnp.maximum(stat[...], _lanes(jnp.maximum, s))

    top = jnp.max(stat[...], axis=1, keepdims=True) * scale2
    stat[...] = jnp.zeros_like(stat)

    @pl.loop(lo, hi)
    def _(j):
        e = jnp.exp2(strip[:, cols(j)] * scale2 - top)
        strip[:, cols(j)] = e
        stat[...] += _lanes(jnp.add, e)

    total = jnp.sum(stat[...], axis=1, keepdims=True)
    inv = 1.0 / total

    def body(j, acc):
        p = (strip[:, cols(j)] * inv).astype(jnp.bfloat16)
        return acc + jnp.dot(p, v_scr[cols(j), :], preferred_element_type=jnp.float32)

    acc = lax.fori_loop(lo, hi, body, jnp.zeros((BQ, head_dim), jnp.float32))
    o_ref[...] = acc.astype(jnp.bfloat16)
    lse_ref[...] = top + jnp.log2(total)


def attn_fwd(qkv, start, lo):
    tokens = qkv.shape[0]
    head_dim = qkv.shape[1] // 3
    return pl.pallas_call(
        functools.partial(attn_fwd_kernel, head_dim),
        grid_spec=pltpu.PrefetchScalarGridSpec(
            num_scalar_prefetch=1,
            grid=(tokens // BQ,),
            in_specs=[pl.BlockSpec(qkv.shape, lambda i, lo: (0, 0)),
                      pl.BlockSpec((BQ, 1), lambda i, lo: (i, 0))],
            out_specs=[pl.BlockSpec((BQ, head_dim), lambda i, lo: (i, 0)),
                       pl.BlockSpec((BQ, 1), lambda i, lo: (i, 0))],
            scratch_shapes=[pltpu.VMEM((tokens, head_dim), jnp.bfloat16),
                            pltpu.VMEM((tokens, head_dim), jnp.bfloat16),
                            pltpu.VMEM((BQ, tokens), jnp.float32),
                            pltpu.VMEM((BQ, 128), jnp.float32)]),
        out_shape=[jax.ShapeDtypeStruct((tokens, head_dim), jnp.bfloat16),
                   jax.ShapeDtypeStruct((tokens, 1), jnp.float32)],
        compiler_params=pltpu.CompilerParams(vmem_limit_bytes=VMEM_LIMIT),
        cost_estimate=pl.CostEstimate(flops=4 * tokens * tokens * head_dim, bytes_accessed=4 * tokens * 1024,
                                      transcendentals=0),
        name="attn_fwd",
    )(lo, qkv, start)


def attn_bwd_kernel(head_dim, lo_ref, qkv_ref, do_ref, start_ref, lse_ref, out_ref,
                    k_scr, v_scr, p_strip, g_strip, stat, dk_scr, dv_scr):
    i = pl.program_id(0)
    scale = head_dim ** -0.5
    scale2 = scale * math.log2(math.e)

    @pl.when(i == 0)
    def _():
        k_scr[...] = qkv_ref[:, head_dim:2 * head_dim]
        v_scr[...] = qkv_ref[:, 2 * head_dim:3 * head_dim]
        dk_scr[...] = jnp.zeros_like(dk_scr)
        dv_scr[...] = jnp.zeros_like(dv_scr)

    rows = pl.ds(pl.multiple_of(i * BQ, BQ), BQ)
    q = qkv_ref[rows, 0:head_dim]
    do = do_ref[...]
    start = start_ref[...]
    lse = lse_ref[...]
    lo = lo_ref[i]
    hi = (i * BQ + BQ - 1) // BK + 1

    def cols(j):
        return pl.ds(pl.multiple_of(j * BK, BK), BK)

    stat[...] = jnp.zeros_like(stat)

    @pl.loop(lo, hi)
    def _(j):
        s = _kdot(q, k_scr[cols(j), :])
        p = jnp.where(_mask(i, j, start), jnp.exp2(s * scale2 - lse), 0.0)
        g = _kdot(do, v_scr[cols(j), :]).astype(jnp.bfloat16)
        p_strip[:, cols(j)] = p
        g_strip[:, cols(j)] = g
        stat[...] += _lanes(jnp.add, p * g.astype(jnp.float32))

    mean = jnp.sum(stat[...], axis=1, keepdims=True)
    q_t = q.astype(jnp.float32).T.astype(jnp.bfloat16)
    do_t = do.astype(jnp.float32).T.astype(jnp.bfloat16)

    def body(j, acc):
        p = p_strip[:, cols(j)]
        ds = (p * (g_strip[:, cols(j)].astype(jnp.float32) - mean)).astype(jnp.bfloat16)
        dk_scr[:, cols(j)] += jnp.dot(q_t, ds, preferred_element_type=jnp.float32)
        dv_scr[:, cols(j)] += jnp.dot(do_t, p.astype(jnp.bfloat16), preferred_element_type=jnp.float32)
        return acc + jnp.dot(ds, k_scr[cols(j), :], preferred_element_type=jnp.float32)

    dq = lax.fori_loop(lo, hi, body, jnp.zeros((BQ, head_dim), jnp.float32))
    out_ref[rows, 0:head_dim] = (dq * scale).astype(jnp.bfloat16)

    @pl.when(i == pl.num_programs(0) - 1)
    def _():
        @pl.loop(0, dk_scr.shape[1] // BK)
        def _(j):
            out_ref[cols(j), head_dim:2 * head_dim] = (dk_scr[:, cols(j)] * scale).T.astype(jnp.bfloat16)
            out_ref[cols(j), 2 * head_dim:3 * head_dim] = dv_scr[:, cols(j)].T.astype(jnp.bfloat16)


def attn_bwd(qkv, d_out, start, lse, lo):
    tokens = qkv.shape[0]
    head_dim = qkv.shape[1] // 3
    return pl.pallas_call(
        functools.partial(attn_bwd_kernel, head_dim),
        grid_spec=pltpu.PrefetchScalarGridSpec(
            num_scalar_prefetch=1,
            grid=(tokens // BQ,),
            in_specs=[pl.BlockSpec(qkv.shape, lambda i, lo: (0, 0)),
                      pl.BlockSpec((BQ, head_dim), lambda i, lo: (i, 0)),
                      pl.BlockSpec((BQ, 1), lambda i, lo: (i, 0)),
                      pl.BlockSpec((BQ, 1), lambda i, lo: (i, 0))],
            out_specs=pl.BlockSpec(qkv.shape, lambda i, lo: (0, 0)),
            scratch_shapes=[pltpu.VMEM((tokens, head_dim), jnp.bfloat16),
                            pltpu.VMEM((tokens, head_dim), jnp.bfloat16),
                            pltpu.VMEM((BQ, tokens), jnp.float32),
                            pltpu.VMEM((BQ, tokens), jnp.bfloat16),
                            pltpu.VMEM((BQ, 128), jnp.float32),
                            pltpu.VMEM((head_dim, tokens), jnp.float32),
                            pltpu.VMEM((head_dim, tokens), jnp.float32)]),
        out_shape=jax.ShapeDtypeStruct(qkv.shape, jnp.bfloat16),
        compiler_params=pltpu.CompilerParams(vmem_limit_bytes=VMEM_LIMIT),
        cost_estimate=pl.CostEstimate(flops=10 * tokens * tokens * head_dim, bytes_accessed=4 * tokens * 1024,
                                      transcendentals=0),
        name="attn_bwd",
    )(lo, qkv, d_out, start, lse)


def segment_starts(seg):
    bounds = [jnp.sum((seg < value).astype(jnp.int32)) for value in (1, 2, 3)]
    start = jnp.where(seg >= 3, bounds[2], jnp.where(seg >= 2, bounds[1], jnp.where(seg >= 1, bounds[0], 0)))
    return start[:, None], start[::BQ] // BK


def solution(mesh):
    groups = mesh.shape["model"]

    def normalize(values):
        values_f32 = values.astype(jnp.float32)
        centered = values_f32 - jnp.mean(values_f32, axis=-1, keepdims=True)
        inv_std = lax.rsqrt(jnp.mean(centered * centered, axis=-1, keepdims=True) + LN_EPS)
        return centered * inv_std, inv_std

    def norm_backward(grad_out, x_hat, inv_std, gain_vec):
        d_gain = jnp.sum(grad_out * x_hat, axis=0)
        d_hat = grad_out * gain_vec.astype(jnp.float32)
        d_in = inv_std * (d_hat - jnp.mean(d_hat, axis=-1, keepdims=True)
                          - x_hat * jnp.mean(d_hat * x_hat, axis=-1, keepdims=True))
        return d_in, d_gain

    def mm(spec, left, right):
        return jnp.einsum(spec, left, right, preferred_element_type=jnp.float32)

    def gather(rows):
        return lax.all_gather(rows, "model", axis=0, tiled=True)

    def scatter(rows):
        return lax.psum_scatter(rows, "model", scatter_dimension=0, tiled=True)

    def local_layer(act_x, seg_ids, gain_one, gain_two, w_qkv, w_out, w_up, w_down, grad_y):
        bf16 = jnp.bfloat16
        tokens, width = act_x.shape
        own = tokens // groups
        here = lax.axis_index("model") * own
        start, lo = segment_starts(seg_ids)
        w_out_all = gather(w_out.reshape(-1, width))

        normed_one, qkv = ln_qkv(act_x, gain_one, w_qkv)
        attn, lse = attn_fwd(qkv, start, lo)
        attn_own = lax.all_to_all(attn, "model", split_axis=0, concat_axis=1, tiled=True)
        x_own = lax.dynamic_slice_in_dim(act_x, here, own)
        dy_own = lax.dynamic_slice_in_dim(grad_y, here, own)
        resid_own = (x_own.astype(jnp.float32) + mm("sc,ce->se", attn_own, w_out_all)).astype(bf16)
        hat_two, inv_two = normalize(resid_own)
        normed_two = gather((hat_two * gain_two.astype(jnp.float32)).astype(bf16))

        act_vals, gelu_pull = jax.vjp(functools.partial(jax.nn.gelu, approximate=True),
                                      mm("sh,hf->sf", normed_two, w_up))
        hidden = act_vals.astype(bf16)
        d_hidden = mm("se,fe->sf", grad_y, w_down).astype(bf16)
        d_pre = gelu_pull(d_hidden.astype(jnp.float32))[0].astype(bf16)
        d_normed_two = scatter(mm("sf,hf->sh", d_pre, w_up).astype(bf16)).astype(jnp.float32)
        d_in_two, d_gain_two = norm_backward(d_normed_two, hat_two, inv_two, gain_two)
        d_resid = (dy_own.astype(jnp.float32) + d_in_two).astype(bf16)
        d_attn_own = mm("se,ce->sc", d_resid, w_out_all).astype(bf16)
        d_attn = lax.all_to_all(d_attn_own, "model", split_axis=1, concat_axis=0, tiled=True)

        sum_two = scatter(mm("sf,fe->se", hidden, w_down).astype(bf16))
        layer_out = gather((resid_own.astype(jnp.float32) + sum_two.astype(jnp.float32)).astype(bf16))

        d_qkv = attn_bwd(qkv, d_attn, start, lse, lo)
        d_normed_one = scatter(mm("sc,hc->sh", d_qkv, w_qkv).astype(bf16)).astype(jnp.float32)
        hat_one, inv_one = normalize(x_own)
        d_in_one, d_gain_one = norm_backward(d_normed_one, hat_one, inv_one, gain_one)
        grad_x = gather((d_resid.astype(jnp.float32) + d_in_one).astype(bf16))
        d_gains = lax.psum(jnp.stack([d_gain_one, d_gain_two]), "model").astype(bf16)

        d_wout = mm("sd,se->de", attn, gather(d_resid)).astype(bf16).reshape(w_out.shape)
        d_down = mm("sf,se->fe", hidden, grad_y).astype(bf16)
        d_up = mm("sh,sf->hf", normed_two, d_pre).astype(bf16)
        d_wqkv = mm("sh,sc->hc", normed_one, d_qkv).astype(bf16)
        return layer_out, grad_x, d_wqkv, d_wout, d_up, d_down, d_gains[0], d_gains[1]

    in_specs = (P("data", None), P("data"), P(None), P(None), P(None, "model"),
                P("model", None, None), P(None, "model"), P("model", None), P("data", None))
    out_specs = (P("data", None), P("data", None), P("data", "model"), P(("data", "model"), None, None),
                 P("data", "model"), P(("data", "model"), None), P("data"), P("data"))
    return jax.shard_map(local_layer, mesh=mesh, in_specs=in_specs, out_specs=out_specs, check_vma=False)
```

time: 1050 us -> 844 us (0.80)
  other arithmetic: 228 us -> 16.9 us
  matrix products: 242 us -> 95.4 us
  Pallas kernels: 0 us -> 88.5 us
  blocking collectives: 0 us -> 65.1 us
  waiting for transfers between devices: 541 us -> 505 us
  local copies, waits for them, and re-layouts: 11.7 us -> 35.2 us
    psum x3 -> x0, waiting for transfers between devices: 541 us -> none  [the longest x1 215 us: local_layer(): sum_two = lax.psum(part_two, 'model')]
    reduce_scatter x0 -> x3, waiting for transfers between devices: none -> 302 us  [scatter(): return lax.psum_scatter(rows, 'model', scatter_dimension=0, tiled=True)]
    all_gather x0 -> x5, waiting for transfers between devices: none -> 189 us  [gather(): return lax.all_gather(rows, 'model', axis=0, tiled=True)]
    dot_general x18 -> x11, matrix products: 242 us -> 95.4 us  [mm(): return jnp.einsum(spec, left, right, preferred_element_type=jnp.float32)]
    convert_element_type x8 -> x5, other arithmetic: 135 us -> 6.27 us  [the longest x1 2.7 us: local_layer(): d_resid = (dy_own.astype(jnp.float32) + d_in_two).astype(bf16)]
    pallas_call x0 -> x3, Pallas kernels: none -> 88.5 us  [the longest x1 38 us: attn_bwd(): pl.pallas_call(functools.partial(attn_bwd_kernel, head_dim), grid_spec=pl...]
    psum x0 -> x1, blocking collectives: none -> 47.8 us  [local_layer(): lax.psum(jnp.stack([d_gain_one, d_gain_two]), 'model').astype(bf16)]
    reduce_sum x2, other arithmetic: 37.2 us -> 3.17 us  [norm_backward(): d_gain = jnp.sum(grad_out * x_hat, axis=0)]
  transfers between devices with their start and end apart: 3 -> 9, of which waited for: 3 -> 7; matrix products, arithmetic and copies ran while one was open for 4% -> 8% of each run, Pallas kernels for 0% -> 6%
where the time goes in v1:
time: 844 us; the launch traced here: 831 us
  waiting for transfers between devices  505 us (60%)
  matrix products  95.4 us (11%)
  Pallas kernels  88.5 us (10%)
  blocking collectives  65.1 us (8%)
  local copies, waits for them, and re-layouts  35.2 us (4%)
  other arithmetic  16.9 us (2%)
  between operations  14.6 us (2%)
  starting transfers between devices  10.6 us (1%)
    reduce_scatter x3, waiting for transfers between devices, scatter(): return lax.psum_scatter(rows, 'model', scatter_dimension=0, tiled=True)  302 us
    all_gather x5, waiting for transfers between devices, gather(): return lax.all_gather(rows, 'model', axis=0, tiled=True)  189 us
    dot_general x11, matrix products, mm(): return jnp.einsum(spec, left, right, preferred_element_type=jnp.float32)  95.4 us
    psum x1, blocking collectives, local_layer(): lax.psum(jnp.stack([d_gain_one, d_gain_two]), 'model').astype(bf16)  47.8 us
    pallas_call x1, Pallas kernels, attn_bwd(): pl.pallas_call(functools.partial(attn_bwd_kernel, head_dim), grid_spec=pl...  38 us
    pallas_call x1, Pallas kernels, attn_fwd(): pl.pallas_call(functools.partial(attn_fwd_kernel, head_dim), grid_spec=pl...  31.4 us
    unnamed x39, local copies, waits for them, and re-layouts  27.3 us
    pallas_call x1, Pallas kernels, ln_qkv(): pl.pallas_call(ln_qkv_kernel, grid=(tokens // rows,), in_specs=[pl.BlockS...  19.1 us
  transfers between devices with their start and end apart: 9, of which 7 were waited for; matrix products, arithmetic and copies ran while one was open for 8% of the time, Pallas kernels for 6%

profile of v1, /device:TPU:97, one launch (start us, length us, event | category | flops | bytes accessed | tf_op | source)
XLA Modules:
  0.0 831.3 jit_solution(490300894306960222)
XLA Ops:
  10.7 2.7 select_select_fusion
  13.4 2.2 copy.19.w_ref
  18.1 19.1 %ln_qkv.1 = (bf16[4096,2048]{1,0:T(8,128)(2,1)}, bf16[4096,192]{1,0:T(8,128)(2,1)}) custom-call(bf16[4096,2048]{1,0:T(8,128)(2,1)} %x_ref.1, bf16[1,2048]{1,0:T(2,128)(2,1)} %broadcast_in_dim.36.g_ref, bf16[2048,192]{1,0:T(8,128)(2,1)} %copy.19.w_ref), custom_call_target="tpu_custom_call" | custom-call | flops 3221225472 | bytes 33554432 | tf_op jit(solution)/shard_map/ln_qkv/pallas_call | solution.py:30
  37.2 31.4 %attn_fwd.1 = (bf16[4096,64]{1,0:T(8,128)(2,1)}, f32[4096,1]{1,0:T(8,128)}) custom-call(s32[16]{0:T(128)} %and_select_fusion.lo_ref, bf16[4096,192]{1,0:T(8,128)(2,1)} %get-tuple-element.12.qkv_ref, s32[4096,1]{1,0:T(8,128)} %copy.20.start_ref), custom_call_target="tpu_custom_call" | custom-call | flops 4294967296 | bytes 16777216 | tf_op jit(solution)/shard_map/attn_fwd/pallas_call | solution.py:114
  68.6 2.3 copy.21
  71.0 9.1 %all-to-all-start = ((bf16[32,128,64]{1,2,0:T(8,128)(2,1)}), bf16[32,128,64]{1,2,0:T(8,128)(2,1)S(1)}, u32[]{:S(2)}, u32[]{:S(2)}) async-start(bf16[32,128,64]{1,2,0:T(8,128)(2,1)} %copy.21), calls=%async_computation | async-start | bytes 1048576 | tf_op jit(solution)/shard_map/all_to_all | solution.py:262
  80.2 10.9 %all-to-all-done = bf16[32,128,64]{1,2,0:T(8,128)(2,1)S(1)} async-done(((bf16[32,128,64]{1,2,0:T(8,128)(2,1)}), bf16[32,128,64]{1,2,0:T(8,128)(2,1)S(1)}, u32[]{:S(2)}, u32[]{:S(2)}) %all-to-all-start) | async-done | bytes 524320 | tf_op jit(solution)/shard_map/all_to_all | solution.py:262
  91.1 4.8 fusion.49
  97.7 65.8 %all-gather.7.cloned.1.call-done = bf16[4096,2048]{1,0:T(8,128)(2,1)} async-done(((bf16[128,2048]{1,0:T(8,128)(2,1)}), bf16[4096,2048]{1,0:T(8,128)(2,1)}) %all-gather.7.cloned.1.call-update) | async-done | bytes 16777232 | tf_op jit(solution)/shard_map/all_gather | solution.py:247
  163.4 8.1 fusion.50
  171.6 2.0 copy-done.5
  173.5 11.5 %fusion.6 = bf16[4096,256]{1,0:T(8,128)(2,1)} fusion(f32[4096,256]{1,0:T(8,128)S(1)} %fusion.50, bf16[4096,2048]{1,0:T(8,128)(2,1)} %param.17, bf16[256,2048]{1,0:T(8,128)(2,1)S(1)} %copy-done.11), kind=kOutput, calls=%fused_computation.14 | convolution fusion | flops 4318035968 | bytes 24117248 | tf_op jit(solution)/shard_map/se,fe->sf/dot_general | solution.py:244
  185.1 10.1 %convolution_convert_fusion.1 = bf16[4096,2048]{1,0:T(8,128)(2,1)} fusion(bf16[4096,256]{1,0:T(8,128)(2,1)} %fusion.6, bf16[2048,256]{1,0:T(8,128)(2,1)S(1)} %copy-done), kind=kOutput, calls=%fused_computation.1 | convolution fusion | flops 4303355904 | bytes 19922944 | tf_op jit(solution)/shard_map/sf,hf->sh/dot_general | solution.py:244
  195.4 11.0 %convolution_convert_fusion.2 = bf16[4096,2048]{1,0:T(8,128)(2,1)} fusion(bf16[256,2048]{1,0:T(8,128)(2,1)S(1)} %copy-done.11, f32[4096,256]{1,0:T(8,128)} %copy-done.5), kind=kOutput, calls=%fused_computation.2 | convolution fusion | flops 4312793088 | bytes 22020096 | tf_op jit(solution)/shard_map/sf,fe->se/dot_general | solution.py:244
  207.0 93.3 %reduce-scatter.6.cloned.1.call-done = bf16[128,2048]{1,0:T(8,128)(2,1)} async-done(((bf16[4096,2048]{1,0:T(8,128)(2,1)}), bf16[128,2048]{1,0:T(8,128)(2,1)}) %reduce-scatter.6.cloned.1.call-update) | async-done | bytes 524304 | tf_op jit(solution)/shard_map/reduce_scatter | solution.py:250
  301.8 109.0 %reduce-scatter.4.cloned.1.call-done = bf16[128,2048]{1,0:T(8,128)(2,1)} async-done(((bf16[4096,2048]{1,0:T(8,128)(2,1)}), bf16[128,2048]{1,0:T(8,128)(2,1)}) %reduce-scatter.4.cloned.1.call-update) | async-done | bytes 524304 | tf_op jit(solution)/shard_map/reduce_scatter | solution.py:250
  410.8 2.7 fusion.44
  413.5 6.4 fusion.17
  420.2 17.3 %all_to_all.38 = bf16[128,32,64]{0,2,1:T(8,128)(2,1)S(1)} all-to-all(bf16[128,32,64]{0,2,1:T(8,128)(2,1)S(1)} %bitcast.48), channel_id=1, replica_groups=mesh['data'=1,'model'=32] {'model'}, dimensions={1} | all-to-all | bytes 1048576 | tf_op jit(solution)/shard_map/all_to_all | solution.py:278
  438.9 38.0 %attn_bwd.1 = bf16[4096,192]{1,0:T(8,128)(2,1)} custom-call(s32[16]{0:T(128)} %and_select_fusion.lo_ref, bf16[4096,192]{1,0:T(8,128)(2,1)} %get-tuple-element.12.qkv_ref, bf16[4096,64]{1,0:T(8,128)(2,1)} %bitcast.49, s32[4096,1]{1,0:T(8,128)} %copy.20.start_ref, f32[4096,1]{1,0:T(8,128)} %get-tuple-element.14.lse_ref), custom_call_target="tpu_custom_call" | custom-call | flops 10737418240 | bytes 16777216 | tf_op jit(solution)/shard_map/attn_bwd/pallas_call | solution.py:196
  476.9 10.1 %convolution_convert_fusion = bf16[4096,2048]{1,0:T(8,128)(2,1)} fusion(bf16[4096,192]{1,0:T(8,128)(2,1)} %attn_bwd.1, bf16[2048,192]{0,1:T(8,128)(2,1)S(1)} %copy-done.9), kind=kOutput, calls=%fused_computation | convolution fusion | flops 3229614080 | bytes 19136512 | tf_op jit(solution)/shard_map/sc,hc->sh/dot_general | solution.py:244
  491.4 100.1 %reduce-scatter.8.cloned.1.call-done = bf16[128,2048]{1,0:T(8,128)(2,1)} async-done(((bf16[4096,2048]{1,0:T(8,128)(2,1)}), bf16[128,2048]{1,0:T(8,128)(2,1)}) %reduce-scatter.8.cloned.1.call-update) | async-done | bytes 524304 | tf_op jit(solution)/shard_map/reduce_scatter | solution.py:250
  593.2 2.5 fusion.39
  595.8 9.7 %convolution_convert_fusion.5 = bf16[2048,256]{1,0:T(8,128)(2,1)} fusion(bf16[4096,2048]{1,0:T(8,128)(2,1)} %all-gather.7.cloned.1.call-done, bf16[4096,256]{1,0:T(8,128)(2,1)S(1)} %copy-done.10), kind=kOutput, calls=%fused_computation.24 | convolution fusion | flops 4295491584 | bytes 19922944 | tf_op jit(solution)/shard_map/sh,sf->hf/dot_general | solution.py:244
  605.6 9.7 %convolution_convert_fusion.4 = bf16[256,2048]{1,0:T(8,128)(2,1)} fusion(bf16[4096,2048]{1,0:T(8,128)(2,1)} %param.17, f32[4096,256]{1,0:T(8,128)S(1)} %copy-done.6), kind=kOutput, calls=%fused_computation.23 | convolution fusion | flops 4304928768 | bytes 22020096 | tf_op jit(solution)/shard_map/sf,se->fe/dot_general | solution.py:244
  615.3 4.3 convolution_convert_fusion.6
  619.7 47.8 %psum.7 = bf16[2,2048]{1,0:T(2,128)(2,1)S(1)} all-reduce(f32[2,2048]{1,0:T(2,128)S(1)} %pad_maximum_fusion), channel_id=1, replica_groups=mesh['data'=1,'model'=32] {'model'}, use_global_device_ids=true, to_apply=%region_16.17 | all-reduce | flops 4096 | bytes 24576 | tf_op jit(solution)/shard_map/psum | solution.py:288
  668.1 63.7 %all-gather.13.cloned.1.call-done = bf16[4096,2048]{1,0:T(8,128)(2,1)} async-done(((bf16[128,2048]{1,0:T(8,128)(2,1)}), bf16[4096,2048]{1,0:T(8,128)(2,1)}) %all-gather.13.cloned.1.call-update) | async-done | bytes 16777232 | tf_op jit(solution)/shard_map/all_gather | solution.py:247
  731.8 9.5 %fusion.26 = bf16[1,64,2048]{2,1,0:T(8,128)(2,1)} fusion(bf16[4096,64]{1,0:T(8,128)(2,1)S(1)} %copy-done.7, bf16[4096,2048]{1,0:T(8,128)(2,1)} %all-gather.13.cloned.1.call-done), kind=kOutput, calls=%fused_computation.31 | convolution fusion | flops 1073872896 | bytes 17563648 | tf_op jit(solution)/shard_map/sd,se->de/dot_general | solution.py:244
  741.3 59.8 %all-gather.11.cloned.1.call-done = bf16[4096,2048]{1,0:T(8,128)(2,1)} async-done(((bf16[128,2048]{1,0:T(8,128)(2,1)}), bf16[4096,2048]{1,0:T(8,128)(2,1)}) %all-gather.11.cloned.1.call-update) | async-done | bytes 16777232 | tf_op jit(solution)/shard_map/all_gather | solution.py:247
  801.2 15.1 %copy.27 = bf16[4096,2048]{1,0:T(8,128)(2,1)} copy(bf16[4096,2048]{1,0:T(8,128)(2,1)} %all-gather.9.cloned.1.call-done) | data formatting | bytes 33554432
  818.1 6.2 copy.28
  (78 shorter events, 20.2 us)
Async XLA Ops:
  7.2 156.2 %copy-start = (bf16[2048,256]{1,0:T(8,128)(2,1)S(1)}, bf16[2048,256]{1,0:T(8,128)(2,1)}, u32[]{:S(2)}) copy-start(bf16[2048,256]{1,0:T(8,128)(2,1)} %param.15) | copy-start | bytes 3145732
  7.2 83.9 %all-gather.15.cloned.1.call-start = ((), (), s32[]{:S(2)}) async-start(), calls=%async_computation.12 | async-start | bytes 8650752 | tf_op jit(solution)/shard_map/all_gather | solution.py:247
  37.2 42.9 %copy-start.13 = (bf16[2048]{0:T(1024)(128)(2,1)S(1)}, bf16[2048]{0:T(1024)(128)(2,1)}, u32[]{:S(2)}) copy-start(bf16[2048]{0:T(1024)(128)(2,1)} %param.12) | copy-start | bytes 12292
  71.0 20.2 %all-to-all-start = ((bf16[32,128,64]{1,2,0:T(8,128)(2,1)}), bf16[32,128,64]{1,2,0:T(8,128)(2,1)S(1)}, u32[]{:S(2)}, u32[]{:S(2)}) async-start(bf16[32,128,64]{1,2,0:T(8,128)(2,1)} %copy.21), calls=%async_computation | async-start | bytes 1048576 | tf_op jit(solution)/shard_map/all_to_all | solution.py:262
  80.1 83.3 %all-gather.7.cloned.1.call-start = ((), (), s32[]{:S(2)}) async-start(), calls=%async_computation.5 | async-start | bytes 17301504 | tf_op jit(solution)/shard_map/all_gather | solution.py:247
  97.3 76.3 %copy-start.11 = (bf16[256,2048]{1,0:T(8,128)(2,1)S(1)}, bf16[256,2048]{1,0:T(8,128)(2,1)}, u32[]{:S(2)}) copy-start(bf16[256,2048]{1,0:T(8,128)(2,1)} %param.16) | copy-start | bytes 3145732
  97.3 203.0 %reduce-scatter.6.cloned.1.call-start = ((), (), s32[]{:S(2)}) async-start(), calls=%async_computation.8 | async-start | bytes 17301504 | tf_op jit(solution)/shard_map/reduce_scatter | solution.py:250
  171.6 2.0 copy-start.5
  195.3 215.5 %reduce-scatter.4.cloned.1.call-start = ((), (), s32[]{:S(2)}) async-start(), calls=%async_computation.6 | async-start | bytes 17301504 | tf_op jit(solution)/shard_map/reduce_scatter | solution.py:250
  206.4 385.1 %reduce-scatter.8.cloned.1.call-start = ((), (), s32[]{:S(2)}) async-start(), calls=%async_computation.9 | async-start | bytes 17301504 | tf_op jit(solution)/shard_map/reduce_scatter | solution.py:250
  413.5 6.5 copy-start.3
  438.9 38.0 %copy-start.9 = (bf16[2048,192]{0,1:T(8,128)(2,1)S(1)}, bf16[2048,192]{0,1:T(8,128)(2,1)}, u32[]{:S(2)}) copy-start(bf16[2048,192]{0,1:T(8,128)(2,1)} %param.13) | copy-start | bytes 2359300
  487.0 1.8 copy-start.12
  487.0 106.2 %copy-start.4 = (bf16[128,2048]{1,0:T(8,128)(2,1)S(1)}, bf16[128,2048]{1,0:T(8,128)(2,1)}, u32[]{:S(2)}) copy-start(bf16[128,2048]{1,0:T(8,128)(2,1)} %copy-done.3) | copy-start | bytes 1572868
  487.1 108.7 %copy-start.10 = (bf16[4096,256]{1,0:T(8,128)(2,1)S(1)}, bf16[4096,256]{1,0:T(8,128)(2,1)}, u32[]{:S(2)}) copy-start(bf16[4096,256]{1,0:T(8,128)(2,1)} %fusion.6) | copy-start | bytes 6291460
  487.1 181.0 %all-gather.9.cloned.1.call-start = ((), (), s32[]{:S(2)}) async-start(), calls=%async_computation.7 | async-start | bytes 17301504 | tf_op jit(solution)/shard_map/all_gather | solution.py:247
  487.7 244.1 %all-gather.13.cloned.1.call-start = ((), (), s32[]{:S(2)}) async-start(), calls=%async_computation.11 | async-start | bytes 17301504 | tf_op jit(solution)/shard_map/all_gather | solution.py:247
  488.5 312.6 %all-gather.11.cloned.1.call-start = ((), (), s32[]{:S(2)}) async-start(), calls=%async_computation.10 | async-start | bytes 17301504 | tf_op jit(solution)/shard_map/all_gather | solution.py:247
  595.8 9.7 %copy-start.6 = (f32[4096,256]{1,0:T(8,128)S(1)}, f32[4096,256]{1,0:T(8,128)}, u32[]{:S(2)}) copy-start(f32[4096,256]{1,0:T(8,128)} %copy-done.5) | copy-start | bytes 12582916
  595.8 19.5 %slice-start = ((s8[16777216]{0:T(1024)(128)(4,1)}), s8[4194304]{0:T(1024)(128)(4,1)S(1)}, s32[]{:S(2)}) async-start(s8[16777216]{0:T(1024)(128)(4,1)} %bitcast.53), calls=%async_computation.13 | async-start | bytes 8388608
  595.8 19.4 %slice-start.1 = ((s8[16777216]{0:T(1024)(128)(4,1)}), s8[4194304]{0:T(1024)(128)(4,1)S(1)}, s32[]{:S(2)}) async-start(s8[16777216]{0:T(1024)(128)(4,1)} %bitcast.53), calls=%async_computation.14 | async-start | bytes 8388608
  595.8 19.4 %slice-start.2 = ((s8[16777216]{0:T(1024)(128)(4,1)}), s8[4194304]{0:T(1024)(128)(4,1)S(1)}, s32[]{:S(2)}) async-start(s8[16777216]{0:T(1024)(128)(4,1)} %bitcast.53), calls=%async_computation.15 | async-start | bytes 8388608
  605.5 9.7 %copy-start.8 = (bf16[4096,192]{1,0:T(8,128)(2,1)S(1)}, bf16[4096,192]{1,0:T(8,128)(2,1)}, u32[]{:S(2)}) copy-start(bf16[4096,192]{1,0:T(8,128)(2,1)} %attn_bwd.1) | copy-start | bytes 4718596
  605.6 9.7 %slice-start.3 = ((s8[16777216]{0:T(1024)(128)(4,1)}), s8[4194304]{0:T(1024)(128)(4,1)S(1)}, s32[]{:S(2)}) async-start(s8[16777216]{0:T(1024)(128)(4,1)} %bitcast.53), calls=%async_computation.16 | async-start | bytes 8388608
  615.3 116.5 %copy-start.7 = (bf16[4096,64]{1,0:T(8,128)(2,1)S(1)}, bf16[4096,64]{1,0:T(8,128)(2,1)}, u32[]{:S(2)}) copy-start(bf16[4096,64]{1,0:T(8,128)(2,1)} %get-tuple-element.13) | copy-start | bytes 1572868
  801.2 16.9 %copy-start.2 = (bf16[4096,2048]{1,0:T(8,128)(2,1)S(1)}, bf16[4096,2048]{1,0:T(8,128)(2,1)}, u32[]{:S(2)}) copy-start(bf16[4096,2048]{1,0:T(8,128)(2,1)} %all-gather.11.cloned.1.call-done) | copy-start | bytes 50331652
  818.1 6.2 copy-start.1
Sparse Core Ops, SparseCore 0:
  10.1 51.6 all-gather.14
  97.4 65.9 all-gather.6
  195.4 104.8 reduce-scatter.5
  303.9 106.8 reduce-scatter.3
  487.2 104.2 reduce-scatter.7
  593.4 69.8 all-gather.8
  665.4 66.3 all-gather.12
  734.5 66.6 all-gather.10
